TPU v7x, 32 devices: a whole 2x2x4 slice. The times are simulated.
32 devices in a mesh: curve: 8 (over z, x), grp: 4 (over y, core).
Axes of the slice: x: 2, y: 2, z: 4, core: 2. Of those that a mesh axis runs over, the one named last changes fastest.
Arguments:
- state: float32 [2, 512, 4, 12288], P(None, None, 'grp', 'curve'), may hold values from -6 to 6
- coef: float32 [512, 4, 12288], P(None, 'grp', 'curve'), may hold values from 0.2 to 4
- counts: int32 [4, 8], P('grp', 'curve'), may hold values from 512 to 1536, as said below
Outputs:
- smoothed: float32 [512, 4, 8192], P(None, 'grp', 'curve')
Inputs may be any that keep to these rules, and one draw needn't show every extreme that they name: `counts`: each rank's count is 1024 plus the drift at its own end minus the drift at the end of the rank before it; drifts lie in -256 to 256, are zero before the first rank and at the last rank, so the curve holds 8192 blocks; in every curve one rank holds exactly 1536 blocks.
All inputs are finite; a program needn't handle non-finite values.
Results may differ from a plain program's by a relative error of at most 0.00002.
Values sent between devices are 32-bit elements; how exact they have to be, the bound alone decides.
A program may use at most 128 MiB of HBM per device.

v0:
```python
import functools

import jax
import jax.numpy as jnp
from jax import lax
from jax.experimental import pallas as pl
from jax.experimental.pallas import tpu as pltpu
from jax.sharding import PartitionSpec as P

AVG = 1024
HALF = 256
LANES = 128
SIDE = 8
PAD = 8
WIDE = 16
LEAD = 4
MESH = pl.DeviceIdType.MESH


def exchange(
    n, groups, cap_rows, counts, mine, state, coef, out, every, every_s, ends, met, ghost, raw0, raw1, raw2, wide0, wide1, source,
    inverse, out0, out1, out2, out3, in0, in1, in2, in3, face0, face1, near0, near1, inv, first_fix,
    second_fix, result, edge_out, edge_in, count_send, count_recv, end_send, end_recv, local_sem, load_sem, send_sem, recv_sem, face_send, face_recv, out_sem,
):
    cells = SIDE * SIDE * SIDE
    own_rows = AVG // LANES
    half_rows = HALF // LANES
    rank, group = lax.axis_index("curve"), lax.axis_index("grp")
    has_left, has_right = rank > 0, rank < n - 1
    has_low, has_high = group > 0, group < groups - 1
    sides = (
        (has_left, {"curve": rank - 1}), (has_right, {"curve": rank + 1}),
        (has_low, {"grp": group - 1}), (has_high, {"grp": group + 1}),
    )
    raw = (raw0, raw1, raw2)
    loads = []
    for f, src in ((0, state.at[0]), (2, coef), (1, state.at[1])):
        load = pltpu.make_async_copy(src, raw[f].at[pl.ds(PAD, cells * cap_rows)], load_sem.at[f])
        load.start()
        loads.append((f, load))
    loads = dict(loads)
    barrier = pltpu.get_barrier_semaphore()
    for there, device in sides:
        @pl.when(there)
        def _():
            pl.semaphore_signal(barrier, inc=1, device_id=device, device_id_type=MESH)
    for off in range(2, n - 1):
        peer = lax.rem(rank + off, n)
        pl.semaphore_signal(barrier, inc=1, device_id={"curve": peer}, device_id_type=MESH)
    for there, peer in ((has_left, n - 1), (has_right, 0)):
        @pl.when(jnp.logical_not(there))
        def _():
            pl.semaphore_signal(barrier, inc=1, device_id={"curve": peer}, device_id_type=MESH)
    pl.semaphore_wait(barrier, n - 1 + has_low.astype(jnp.int32) + has_high.astype(jnp.int32))

    tallies = []
    for off in range(1, n):
        tallies.append(
            pltpu.make_async_remote_copy(
                src_ref=mine, dst_ref=every.at[rank], send_sem=count_send.at[off],
                recv_sem=count_recv.at[off], device_id={"curve": lax.rem(rank + off, n)},
                device_id_type=MESH,
            )
        )
        tallies[-1].start()
    keep = pltpu.make_async_copy(mine, every.at[rank], local_sem.at[0])
    keep.start()
    lane = lax.broadcasted_iota(jnp.int32, (8, LANES), 1)
    row = lax.broadcasted_iota(jnp.int32, (8, LANES), 0)
    held = counts[0, 0]
    last = jnp.clip(held - 1, 0, cap_rows * LANES - 1)
    last_row = lax.shift_right_logical(last, 7)
    last_turn = (LANES - (last & (LANES - 1))) & (LANES - 1)
    for f in range(3):
        loads[f].wait()
    for side, at, turn, outer_x, near_x in ((0, 0, 0, 1, 0), (1, last_row, last_turn, SIDE - 2, SIDE - 1)):
        packed = jnp.zeros((8, LANES), jnp.float32)
        for p, (f, x) in enumerate(((0, outer_x), (0, near_x), (1, near_x), (2, near_x))):
            for y in range(SIDE):
                base = (x * (SIDE * SIDE) + y * SIDE) * cap_rows + PAD + at
                value = raw[f][pl.ds(base, 8, stride=cap_rows), :]
                if f == 2:
                    value = 1.0 / (6.0 + value)
                spot = p * SIDE + y
                if side:
                    value = pltpu.roll(value, (turn + spot) & (LANES - 1), 1)
                elif spot:
                    value = pltpu.roll(value, spot, 1)
                packed = jnp.where(lane == spot, value, packed)
        ends[side] = packed

    def greeted(side):
        return pltpu.make_async_remote_copy(
            src_ref=ends.at[side], dst_ref=met.at[1 - side], send_sem=end_send.at[side],
            recv_sem=end_recv.at[side], device_id=sides[side][1], device_id_type=MESH,
        )

    for side in range(2):
        @pl.when(sides[side][0])
        def _():
            greeted(side).start()
    keep.wait()
    for copy in tallies:
        copy.wait()
    keep = pltpu.make_async_copy(every, every_s, local_sem.at[1])
    keep.start()
    keep.wait()
    before = 0
    for r in range(n):
        before = before + jnp.where(r < rank, every_s[r, 0, 0], 0)
    drift_prev = jnp.clip(before - rank * AVG, -HALF, HALF)
    drift_next = drift_prev + held - AVG
    shift = 8 * LANES - LEAD * LANES - drift_prev
    first = lax.shift_right_logical(shift, 7) - 8 + PAD
    part = shift & (LANES - 1)
    turn = (LANES - part) & (LANES - 1)
    stay = lane >= part
    low_rows, high_rows = pl.ds(0, 8), pl.ds(8, 8)
    own = pl.ds(LEAD, own_rows)
    to_left, to_right = 2, LEAD + own_rows - 8
    zero = jnp.zeros((8, LANES), jnp.float32)

    def each(fn):
        @pl.loop(0, SIDE)
        def _(x):
            @pl.loop(0, SIDE)
            def _(y):
                fn(x, y)

    def aligned(f, x, y, z, half):
        base = (x * (SIDE * SIDE) + y * SIDE + z) * cap_rows + first + 8 * half
        low, high = raw[f][pl.ds(base, 8), :], raw[f][pl.ds(base + 1, 8), :]
        return pltpu.roll(jnp.where(stay, low, high), turn, 1)

    kinds = ((out0, in0), (out1, in1), (out2, in2), (out3, in3))

    def sent(kind, side):
        return pltpu.make_async_remote_copy(
            src_ref=kinds[kind][0].at[side], dst_ref=kinds[kind][1].at[1 - side],
            send_sem=send_sem.at[2 * kind + side], recv_sem=recv_sem.at[2 * kind + side],
            device_id=sides[side][1], device_id_type=MESH,
        )

    def send(kind):
        @pl.when(has_right)
        def _():
            sent(kind, 1).start()

        @pl.when(has_left)
        def _():
            sent(kind, 0).start()

    def arrived(kind):
        @pl.when(has_left)
        def _():
            sent(kind, 1).wait_recv()

        @pl.when(has_right)
        def _():
            sent(kind, 0).wait_recv()

    def pack(put, get, planes):
        @pl.loop(0, SIDE)
        def _(x):
            for p, y in enumerate(planes):
                for z in range(SIDE):
                    put[0, p, x, z] = get(x, y, z, pl.ds(to_left, half_rows))
                    put[1, p, x, z] = get(x, y, z, pl.ds(8 + to_right, half_rows))

    outer, near_outer = (0, SIDE - 1), (0, 1, SIDE - 2, SIDE - 1)

    def step(x, y):
        for z in range(SIDE):
            wide0[x + 1, y + 1, z, low_rows, :] = aligned(0, x, y, z, 0)
            wide0[x + 1, y + 1, z, high_rows, :] = aligned(0, x, y, z, 1)
    each(step)
    pack(out0, lambda x, y, z, rows: wide0[x + 1, y + 1, z, rows, :], outer)
    send(0)

    def step(x, y):
        for z in range(SIDE):
            inverse[x, y, z, low_rows, :] = 1.0 / (aligned(2, x, y, z, 0) + 6.0)
            inverse[x, y, z, high_rows, :] = 1.0 / (aligned(2, x, y, z, 1) + 6.0)
    each(step)
    pack(out1, lambda x, y, z, rows: inverse[x, y, z, rows, :], near_outer)
    send(1)

    def step(x, y):
        for z in range(SIDE):
            source[x, y, z, low_rows, :] = aligned(1, x, y, z, 0)
            source[x, y, z, high_rows, :] = aligned(1, x, y, z, 1)
    each(step)

    for side in range(2):
        @pl.when(sides[side][0])
        def _():
            greeted(1 - side).wait_recv()
            greeted(side).wait_send()
    keep_ends = pltpu.make_async_copy(met, ghost, local_sem.at[2])
    keep_ends.start()
    keep_ends.wait()
    block = row * LANES + lane - LEAD * LANES
    for side, at, planes in (
        (0, drift_prev - 1, ((wide0, 1, SIDE - 1), (wide0, 1, SIDE), (source, 0, SIDE - 1), (inverse, 0, SIDE - 1))),
        (1, AVG + drift_next, ((wide0, 1, 2), (wide0, 1, 1), (source, 0, 0), (inverse, 0, 0))),
    ):
        here = (block == at, block + 8 * LANES == at)
        for p, (ref, off, x) in enumerate(planes):
            @pl.loop(0, SIDE)
            def _(y):
                for z in range(SIDE):
                    value = jnp.where(sides[side][0], ghost[side, z, p * SIDE + y], 0.0)
                    for half, rows in enumerate((low_rows, high_rows)):
                        old = ref[x, y + off, z, rows, :]
                        ref[x, y + off, z, rows, :] = jnp.where(here[half], value, old)

    def borders(ref):
        @pl.loop(0, SIDE)
        def _(y):
            for z in range(SIDE):
                turned = [pltpu.roll(ref[1, y + 1, z, rows, :], LANES - 1, 1) for rows in (low_rows, high_rows)]
                carry = [pltpu.roll(value, 7, 0) for value in turned]
                carry[0] = jnp.where(row == 7, carry[1], carry[0])
                for half, rows in enumerate((low_rows, high_rows)):
                    ref[SIDE + 1, y + 1, z, rows, :] = jnp.where(lane == LANES - 1, carry[half], turned[half])
                turned = [pltpu.roll(ref[SIDE, y + 1, z, rows, :], 1, 1) for rows in (low_rows, high_rows)]
                carry = [pltpu.roll(value, 1, 0) for value in turned]
                carry[1] = jnp.where(row == 0, carry[0], carry[1])
                for half, rows in enumerate((low_rows, high_rows)):
                    ref[0, y + 1, z, rows, :] = jnp.where(lane == 0, carry[half], turned[half])

        @pl.loop(0, SIDE)
        def _(x):
            for at in (0, SIDE + 1):
                ref[x + 1, at] = jnp.zeros((SIDE, WIDE, LANES), jnp.float32)

    def sweep(ref, put):
        def step(x, y):
            for rows in (low_rows, high_rows):
                line = [ref[x + 1, y + 1, z, rows, :] for z in range(SIDE)]
                for z in range(SIDE):
                    total = ref[x + 2, y + 1, z, rows, :] + ref[x, y + 1, z, rows, :]
                    total = total + (ref[x + 1, y + 2, z, rows, :] + ref[x + 1, y, z, rows, :])
                    if z + 1 < SIDE:
                        total = total + line[z + 1]
                    if z > 0:
                        total = total + line[z - 1]
                    value = (source[x, y, z, rows, :] + total) * inverse[x, y, z, rows, :]
                    put(x, y, z, rows, value)
        each(step)

    def put(x, y, z, rows, value):
        wide1[x + 1, y + 1, z, rows, :] = value
    borders(wide0)
    sweep(wide0, put)
    pack(out2, lambda x, y, z, rows: wide1[x + 1, y + 1, z, rows, :], outer)
    send(2)

    def put(x, y, z, rows, value):
        if rows is low_rows:
            result[x, y, z, pl.ds(0, 8 - LEAD), :] = value[LEAD:]
            out3[0, x, y, z] = value[to_left : to_left + half_rows]
        else:
            result[x, y, z, pl.ds(8 - LEAD, own_rows - 8 + LEAD), :] = value[:to_right]
            out3[1, x, y, z] = value[to_right : to_right + half_rows]
    borders(wide1)
    sweep(wide1, put)

    spot = lax.broadcasted_iota(jnp.int32, (half_rows, LANES), 0) * LANES
    spot = spot + lax.broadcasted_iota(jnp.int32, (half_rows, LANES), 1)
    is_left = spot < drift_prev
    is_right = spot + (AVG - HALF) >= AVG + drift_next

    def merge(kind, to, get, planes):
        got = kinds[kind][1]
        @pl.loop(0, SIDE)
        def _(x):
            for p, y in enumerate(planes):
                for z in range(SIDE):
                    mine = get(x, y, z)
                    to[p, x, z] = mine
                    to[p, x, z, pl.ds(0, half_rows), :] = jnp.where(is_left, got[0, p, x, z], mine[:half_rows])
                    to[p, x, z, pl.ds(own_rows - half_rows, half_rows), :] = jnp.where(
                        is_right, got[1, p, x, z], mine[own_rows - half_rows :]
                    )

    def faces(b):
        face, near = ((face0, near0), (face1, near1))[b]
        down = pltpu.make_async_remote_copy(
            src_ref=face.at[0], dst_ref=near.at[1], send_sem=face_send.at[2 * b],
            recv_sem=face_recv.at[2 * b], device_id=sides[2][1], device_id_type=MESH,
        )
        up = pltpu.make_async_remote_copy(
            src_ref=face.at[1], dst_ref=near.at[0], send_sem=face_send.at[2 * b + 1],
            recv_sem=face_recv.at[2 * b + 1], device_id=sides[3][1], device_id_type=MESH,
        )
        return down, up

    def send_faces(b):
        for (there, _), copy in zip(sides[2:], faces(b)):
            @pl.when(there)
            def _():
                copy.start()
        for (there, _), at in zip(sides[2:], (0, 1)):
            @pl.when(jnp.logical_not(there))
            def _():
                @pl.loop(0, SIDE)
                def _(x):
                    (near0, near1)[b][at, x] = jnp.zeros((SIDE, own_rows, LANES), jnp.float32)

    def take_faces(b):
        down, up = faces(b)
        @pl.when(has_low)
        def _():
            up.wait_recv()

        @pl.when(has_high)
        def _():
            down.wait_recv()

    arrived(0)
    merge(0, face0, lambda x, y, z: wide0[x + 1, y + 1, z, own, :], outer)
    send_faces(0)
    arrived(1)
    merge(1, inv, lambda x, y, z: inverse[x, y, z, own, :], near_outer)
    take_faces(0)

    @pl.loop(0, SIDE)
    def _(x):
        for p, at, inner in ((0, 0, 1), (1, 3, 2)):
            for z in range(SIDE):
                fix = near0[p, x, z] * inv[at, x, z]
                first_fix[p, x + 1, z] = fix
                second_fix[inner, x, z] = fix * inv[inner, x, z]

    def edges(side):
        return pltpu.make_async_remote_copy(
            src_ref=edge_out.at[side], dst_ref=edge_in.at[1 - side],
            send_sem=face_send.at[4 + side], recv_sem=face_recv.at[4 + side],
            device_id=sides[side][1], device_id_type=MESH,
        )

    for p in range(2):
        for z in range(SIDE):
            value = pltpu.roll(first_fix[p, 1, z], LANES - 1, 1)
            carry = pltpu.roll(value, own_rows - 1, 0)
            first_fix[p, SIDE + 1, z] = jnp.where(lane == LANES - 1, carry, value)
            edge_out[0, p, pl.ds(z, 1), :] = carry[own_rows - 1 : own_rows]
            value = pltpu.roll(first_fix[p, SIDE, z], 1, 1)
            carry = pltpu.roll(value, 1, 0)
            first_fix[p, 0, z] = jnp.where(lane == 0, carry, value)
            edge_out[1, p, pl.ds(z, 1), :] = carry[0:1]
    for side in range(2):
        @pl.when(sides[side][0])
        def _():
            edges(side).start()

        @pl.when(jnp.logical_not(sides[side][0]))
        def _():
            edge_in[side] = jnp.zeros((2, SIDE, LANES), jnp.float32)
    send(3)
    arrived(2)
    merge(2, face1, lambda x, y, z: wide1[x + 1, y + 1, z, own, :], outer)

    @pl.loop(0, SIDE)
    def _(x):
        for p in range(2):
            for z in range(SIDE):
                face1[p, x, z] = face1[p, x, z] + first_fix[p, x + 1, z]
    send_faces(1)
    for side in range(2):
        @pl.when(sides[side][0])
        def _():
            edges(1 - side).wait_recv()
    last_spot = (lane == LANES - 1) & (row == own_rows - 1)
    first_spot = (lane == 0) & (row == 0)
    for p in range(2):
        for z in range(SIDE):
            got = jnp.broadcast_to(edge_in[1, p, pl.ds(z, 1), :], (8, LANES))
            first_fix[p, SIDE + 1, z] = jnp.where(last_spot, got, first_fix[p, SIDE + 1, z])
            got = jnp.broadcast_to(edge_in[0, p, pl.ds(z, 1), :], (8, LANES))
            first_fix[p, 0, z] = jnp.where(first_spot, got, first_fix[p, 0, z])
    take_faces(1)

    @pl.loop(0, SIDE)
    def _(x):
        for p, at in ((0, 0), (1, 3)):
            for z in range(SIDE):
                total = near1[p, x, z] + (first_fix[p, x, z] + first_fix[p, x + 2, z])
                if z + 1 < SIDE:
                    total = total + first_fix[p, x + 1, z + 1]
                if z > 0:
                    total = total + first_fix[p, x + 1, z - 1]
                second_fix[at, x, z] = total * inv[at, x, z]

    arrived(3)
    lo, hi = pl.ds(0, half_rows), pl.ds(own_rows - half_rows, half_rows)

    def step(x, y):
        for z in range(SIDE):
            for side, rows, mask in ((0, lo, is_left), (1, hi, is_right)):
                old = result[x, y, z, rows, :]
                result[x, y, z, rows, :] = jnp.where(mask, in3[side, x, y, z], old)
    each(step)

    @pl.loop(0, SIDE)
    def _(x):
        for p, y in enumerate(near_outer):
            for z in range(SIDE):
                result[x, y, z] = result[x, y, z] + second_fix[p, x, z]
    done = pltpu.make_async_copy(result, out, out_sem)
    done.start()
    for b in range(2):
        for (there, _), copy in zip(sides[2:], faces(b)):
            @pl.when(there)
            def _():
                copy.wait_send()
    for side in range(2):
        @pl.when(sides[side][0])
        def _():
            edges(side).wait_send()
            for kind in range(4):
                sent(kind, side).wait_send()
    done.wait()


def local(state, coef, counts):
    n, groups = lax.axis_size("curve"), lax.axis_size("grp")
    cells, cap = state.shape[1], state.shape[3]
    cap_rows, own_rows, half_rows = cap // LANES, AVG // LANES, HALF // LANES
    f32 = jnp.float32
    mine = jnp.broadcast_to(counts, (1, LANES))
    vmem, hbm, smem = (pl.BlockSpec(memory_space=m) for m in (pltpu.VMEM, pl.ANY, pltpu.SMEM))
    side = (SIDE, SIDE)
    packed = [(2, 2) + side, (2, 4) + side, (2, 2) + side, (2, SIDE) + side]
    packed = [shape + (half_rows, LANES) for shape in packed]
    own = (own_rows, LANES)
    shapes = [(cells * cap_rows + 2 * PAD, LANES)] * 3
    shapes += [(SIDE + 2, SIDE + 2, SIDE, WIDE, LANES)] * 2 + [side + (SIDE, WIDE, LANES)] * 2
    shapes += packed + packed + [(2,) + side + own] * 4
    shapes += [(4,) + side + own, (2, SIDE + 2, SIDE) + own, (4,) + side + own, side + (SIDE,) + own]
    shapes += [(2, 2, SIDE, LANES)] * 2
    out = pl.pallas_call(
        functools.partial(exchange, n, groups, cap_rows),
        out_shape=jax.ShapeDtypeStruct((SIDE, SIDE, SIDE, own_rows, LANES), f32),
        in_specs=[smem, vmem, hbm, hbm],
        out_specs=hbm,
        scratch_shapes=[
            pltpu.VMEM((n, 1, LANES), jnp.int32),
            pltpu.SMEM((n, 1, LANES), jnp.int32),
            pltpu.VMEM((2, 8, LANES), f32),
            pltpu.VMEM((2, 8, LANES), f32),
            pltpu.SMEM((2, 8, LANES), f32),
        ]
        + [pltpu.VMEM(shape, f32) for shape in shapes]
        + [pltpu.SemaphoreType.DMA((k,)) for k in (n, n, 2, 2, 3, 3, 8, 8, 6, 6)]
        + [pltpu.SemaphoreType.DMA],
        compiler_params=pltpu.CompilerParams(
            collective_id=0, has_side_effects=True, vmem_limit_bytes=48 * 1024 * 1024
        ),
    )(
        counts, mine, state.reshape(2, cells * cap_rows, LANES),
        coef.reshape(cells * cap_rows, LANES),
    )
    return out.reshape(cells, 1, AVG)


def solution(mesh):
    placed = (P(None, None, "grp", "curve"), P(None, "grp", "curve"), P("grp", "curve"))
    return jax.shard_map(
        local, mesh=mesh, in_specs=placed, out_specs=P(None, "grp", "curve"), check_vma=False
    )
```

profile of v0, /device:TPU:12, one launch (start us, length us, event | category | flops | bytes accessed | tf_op | source)
XLA Modules:
  0.0 65.4 jit_solution(6818404285082681273)
XLA Ops:
  0.7 0.0 copy-start
  0.7 1.9 %copy-done = f32[512,1,1536]{2,1,0:T(1,128)S(1)} copy-done((f32[512,1,1536]{2,1,0:T(1,128)S(1)}, f32[512,1,1536]{2,1,0:T(1,128)}, u32[]{:S(2)}) %copy-start) | copy-done | bytes 3145752
  2.6 61.5 %shard_map.37 = f32[8,8,8,8,128]{4,3,2,1,0:T(8,128)S(1)} custom-call(s32[1,1]{1,0:T(1,128)} %copy.6.counts, s32[1,128]{1,0:T(1,128)S(1)} %broadcast_in_dim.8.mine, f32[2,6144,128]{2,1,0:T(8,128)} %bitcast.7, f32[6144,128]{1,0:T(8,128)S(1)} %bitcast.6), custom_call_target="tpu_custom_call" | custom-call | tf_op jit(solution)/shard_map/pallas_call | solution.py:443
  64.1 1.3 %copy.7 = f32[512,1,1024]{2,1,0:T(1,128)} copy(f32[512,1,1024]{2,1,0:T(1,128)S(1)} %bitcast.5) | data formatting | bytes 4194304
  (1 shorter events, 0.0 us)
Async XLA Ops:
  0.7 1.9 %copy-start = (f32[512,1,1536]{2,1,0:T(1,128)S(1)}, f32[512,1,1536]{2,1,0:T(1,128)}, u32[]{:S(2)}) copy-start(f32[512,1,1536]{2,1,0:T(1,128)} %param.4) | copy-start | bytes 9437188
where the time goes:
time: 66.4 us; the launch traced here: 65.4 us
  Pallas kernels  61.5 us (93%)
  local copies, waits for them, and re-layouts  3.21 us (5%)
  between operations  0.68 us (1%)
    pallas_call x1, Pallas kernels, local(): pl.pallas_call(functools.partial(exchange, n, groups, cap_rows), out_shap...  61.5 us
    unnamed x3, local copies, waits for them, and re-layouts  3.21 us

commit v1 on v0

v1 whole, which is shorter than its diff:
```python
import functools

import jax
import jax.numpy as jnp
from jax import lax
from jax.experimental import pallas as pl
from jax.experimental.pallas import tpu as pltpu
from jax.sharding import PartitionSpec as P

AVG = 1024
HALF = 256
LANES = 128
SIDE = 8
WIN = HALF // LANES
OWN = AVG // LANES
PAD = 16
FIELD, FACTOR, MIDDLE, FINAL = 0, 2 * SIDE, 6 * SIDE, 8 * SIDE
UNITS = 16 * SIDE
KINDS = 6 + SIDE
MESH = pl.DeviceIdType.MESH


def exchange(
    n, groups, rows, counts, state, coef, out, mine, every, every_s, ends, met, raw0, raw1, raw2, inverse, first,
    second, put, got, face0, face1, near0, near1, inv, fix, change, kept, edge_out, edge_in, count_send, count_recv,
    end_send, end_recv, local_sem, load_sem, send_sem, recv_sem, face_send, face_recv, edge_send, edge_recv,
):
    plane_rows = SIDE * SIDE * rows
    cells_rows = SIDE * plane_rows
    rank, group = lax.axis_index("curve"), lax.axis_index("grp")
    has_left, has_right = rank > 0, rank < n - 1
    has_low, has_high = group > 0, group < groups - 1
    sides = (
        (has_left, {"curve": rank - 1}), (has_right, {"curve": rank + 1}),
        (has_low, {"grp": group - 1}), (has_high, {"grp": group + 1}),
    )
    theres = (has_low, has_high)
    raw = (raw0, raw1, raw2)
    front = (plane_rows, 0, 0)
    loads = {}
    for f, src in ((0, state.at[0]), (2, coef), (1, state.at[1])):
        loads[f] = pltpu.make_async_copy(src, raw[f].at[pl.ds(front[f], cells_rows)], load_sem.at[f])
        loads[f].start()
    barrier = pltpu.get_barrier_semaphore()
    for there, device in sides:
        @pl.when(there)
        def _():
            pl.semaphore_signal(barrier, inc=1, device_id=device, device_id_type=MESH)
    for off in range(2, n - 1):
        peer = lax.rem(rank + off, n)
        pl.semaphore_signal(barrier, inc=1, device_id={"curve": peer}, device_id_type=MESH)
    for there, peer in ((has_left, n - 1), (has_right, 0)):
        @pl.when(jnp.logical_not(there))
        def _():
            pl.semaphore_signal(barrier, inc=1, device_id={"curve": peer}, device_id_type=MESH)

    lane = lax.broadcasted_iota(jnp.int32, (SIDE, LANES), 1)
    level = lax.broadcasted_iota(jnp.int32, (SIDE, LANES), 0)
    held = jnp.clip(counts[0, 0], 2 * HALF, rows * LANES)
    mine[...] = jnp.full((1, LANES), held, jnp.int32)
    last = held - 1
    last_row, last_lane = lax.shift_right_logical(last, 7), last & (LANES - 1)
    tail_row = lax.shift_right_logical(held, 7) - WIN
    tail_part = held & (LANES - 1)
    tail_turn = (LANES - tail_part) & (LANES - 1)
    tail_stay = lane >= tail_part

    def raw_at(f, x, y, r):
        return pl.ds(front[f] + (x * SIDE + y) * (SIDE * rows) + r, SIDE, stride=rows)

    def field_of(x, y, r):
        return raw0[raw_at(0, x, y, r), :]

    def first_at(x, y, r):
        return pl.ds((((x + 1) * SIDE + y) * rows + r) * SIDE, SIDE)

    def flat_at(x, y, r):
        return pl.ds(PAD + ((x * SIDE + y) * rows + r) * SIDE, SIDE)

    def factor_of(x, y, r):
        return 1.0 / (raw2[raw_at(2, x, y, r), :] + 6.0)

    def pack(unit, get, x, y):
        for i in range(WIN):
            put[0, unit, i] = get(x, y, i)
        lines = [get(x, y, tail_row + i) for i in range(WIN + 1)]
        for i in range(WIN):
            put[1, unit, i] = pltpu.roll(jnp.where(tail_stay, lines[i], lines[i + 1]), tail_turn, 1)

    def message(kind):
        if kind < 2:
            return FIELD + kind * SIDE, SIDE
        if kind < 4:
            return FACTOR + (kind - 2) * 2 * SIDE, 2 * SIDE
        if kind < 6:
            return MIDDLE + (kind - 4) * SIDE, SIDE
        return FINAL + (kind - 6) * SIDE, SIDE

    def sent(kind, side):
        start, count = message(kind)
        return pltpu.make_async_remote_copy(
            src_ref=put.at[side, pl.ds(start, count)], dst_ref=got.at[1 - side, pl.ds(start, count)],
            send_sem=send_sem.at[side * KINDS + kind], recv_sem=recv_sem.at[side * KINDS + kind],
            device_id=sides[side][1], device_id_type=MESH,
        )

    def needed(kind, side):
        return sides[side][0] & theres[kind % 2] if kind < 6 else sides[side][0]

    def send(kind):
        for side in range(2):
            @pl.when(needed(kind, side))
            def _():
                sent(kind, side).start()

    def arrived(kind):
        for side in range(2):
            @pl.when(needed(kind, side))
            def _():
                sent(kind, 1 - side).wait_recv()

    outer, inner = (0, SIDE - 1), (1, SIDE - 2)
    loads[0].wait()
    @pl.loop(0, SIDE)
    def _(x):
        for p in range(2):
            pack(FIELD + p * SIDE + x, field_of, x, outer[p])
    loads[2].wait()
    @pl.loop(0, SIDE)
    def _(x):
        for p in range(2):
            for k, y in enumerate((outer[p], inner[p])):
                pack(FACTOR + (2 * p + k) * SIDE + x, factor_of, x, y)
    loads[1].wait()
    for side, at, turn, outer_x, near_x in ((0, 0, 0, 1, 0), (1, last_row, LANES - last_lane, SIDE - 2, SIDE - 1)):
        packed = jnp.zeros((SIDE, LANES), jnp.float32)
        for p, (f, x) in enumerate(((0, outer_x), (0, near_x), (1, near_x), (2, near_x))):
            for y in range(SIDE):
                value = factor_of(x, y, at) if f == 2 else raw[f][raw_at(f, x, y, at), :]
                spot = p * SIDE + y
                value = pltpu.roll(value, (turn + spot) & (LANES - 1), 1)
                packed = jnp.where(lane == spot, value, packed)
        ends[side] = packed

    pl.semaphore_wait(barrier, n - 1 + has_low.astype(jnp.int32) + has_high.astype(jnp.int32))

    def greeted(side):
        return pltpu.make_async_remote_copy(
            src_ref=ends.at[side], dst_ref=met.at[1 - side], send_sem=end_send.at[side],
            recv_sem=end_recv.at[side], device_id=sides[side][1], device_id_type=MESH,
        )

    for side in range(2):
        @pl.when(sides[side][0])
        def _():
            greeted(side).start()
    tallies = []
    for off in range(1, n):
        tallies.append(
            pltpu.make_async_remote_copy(
                src_ref=mine, dst_ref=every.at[rank], send_sem=count_send.at[off],
                recv_sem=count_recv.at[off], device_id={"curve": lax.rem(rank + off, n)},
                device_id_type=MESH,
            )
        )
        tallies[-1].start()
    keep = pltpu.make_async_copy(mine, every.at[rank], local_sem.at[0])
    keep.start()
    for kind in range(4):
        send(kind)

    for side in range(2):
        @pl.when(sides[side][0])
        def _():
            greeted(1 - side).wait_recv()
    shown = [ends[side] for side in range(2)]
    seen = [jnp.where(sides[side][0], met[side], 0.0) for side in range(2)]

    def sums(value):
        above = jnp.where(level < SIDE - 1, pltpu.roll(value, SIDE - 1, 0), 0.0)
        return above + jnp.where(level > 0, pltpu.roll(value, 1, 0), 0.0)

    def borders(get, store, ghosts, spot):
        @pl.loop(0, SIDE // 2)
        def _(half):
            for y in (2 * half, 2 * half + 1):
                turned = [pltpu.roll(get(SIDE - 1, y, r), 1, 1) for r in range(rows)]
                carry = pltpu.roll(ghosts[0], (LANES - spot - y) & (LANES - 1), 1)
                for r in range(rows):
                    store(-1, y, r, jnp.where(lane == 0, carry, turned[r]))
                    carry = turned[r]
                turned = [pltpu.roll(get(0, y, r), LANES - 1, 1) for r in range(rows)]
                ghost = pltpu.roll(ghosts[1], (last_lane + LANES - spot - y) & (LANES - 1), 1)
                for r in range(rows):
                    value = jnp.where(lane == LANES - 1, turned[r + 1], turned[r]) if r + 1 < rows else turned[r]
                    store(SIDE, y, r, jnp.where(lane + r * LANES == last, ghost, value))

    def sweep(get, factor, store):
        @pl.loop(0, SIDE)
        def _(x):
            for r in range(rows):
                line = [get(x, y, r) for y in range(SIDE)]
                for y in range(SIDE):
                    total = (get(x - 1, y, r) + get(x + 1, y, r)) + (raw1[raw_at(1, x, y, r), :] + sums(line[y]))
                    if y > 0:
                        total = total + line[y - 1]
                    if y + 1 < SIDE:
                        total = total + line[y + 1]
                    store(x, y, r, total * factor(x, y, r))

    def store_field(x, y, r, value):
        raw0[raw_at(0, x, y, r), :] = value

    def first_of(x, y, r):
        return first[first_at(x, y, r), :]

    def store_first(x, y, r, value):
        first[first_at(x, y, r), :] = value

    def made_factor(x, y, r):
        value = factor_of(x, y, r)
        inverse[flat_at(x, y, r), :] = value
        return value

    def inverse_of(x, y, r):
        return inverse[flat_at(x, y, r), :]

    def second_of(x, y, r):
        return second[flat_at(x, y, r), :]

    def store_second(x, y, r, value):
        second[flat_at(x, y, r), :] = value

    borders(field_of, store_field, seen, SIDE)
    sweep(field_of, made_factor, store_first)
    @pl.loop(0, SIDE)
    def _(x):
        for p in range(2):
            pack(MIDDLE + p * SIDE + x, first_of, x, outer[p])
    for kind in range(4, 6):
        send(kind)

    def moved(met_end, own_end):
        near = pltpu.roll(met_end, LANES - SIDE, 1)
        total = met_end + pltpu.roll(own_end, LANES - SIDE, 1) + sums(near)
        total = total + jnp.where(lane < SIDE - 1, pltpu.roll(near, LANES - 1, 1), 0.0)
        total = total + jnp.where(lane > 0, pltpu.roll(near, 1, 1), 0.0)
        total = total + pltpu.roll(met_end, LANES - 2 * SIDE, 1)
        return total * pltpu.roll(met_end, LANES - 3 * SIDE, 1)

    seen = [moved(seen[side], shown[side]) for side in range(2)]
    borders(first_of, store_first, seen, 0)
    sweep(first_of, inverse_of, store_second)
    @pl.loop(0, SIDE)
    def _(x):
        for y in range(SIDE):
            pack(FINAL + x * SIDE + y, second_of, x, y)
    for kind in range(6, KINDS):
        send(kind)

    keep.wait()
    for copy in tallies:
        copy.wait()
    keep = pltpu.make_async_copy(every, every_s, local_sem.at[1])
    keep.start()
    keep.wait()
    before = 0
    for r in range(n):
        before = before + jnp.where(r < rank, every_s[r, 0, 0], 0)
    drift_prev = jnp.clip(before - rank * AVG, -HALF, HALF)
    drift_next = jnp.clip(drift_prev + held - AVG, -HALF, HALF)
    base = lax.shift_right_arithmetic(-drift_prev, 7)
    part = (-drift_prev) & (LANES - 1)
    turn = (LANES - part) & (LANES - 1)
    stay = lane >= part
    shift = HALF - jnp.maximum(drift_prev, 0)
    left_part = shift & (LANES - 1)
    left_turn = (LANES - left_part) & (LANES - 1)
    left_pick = (lane >= left_part) & (shift < LANES)
    shift = -HALF - jnp.minimum(drift_next, 0)
    right_part = shift & (LANES - 1)
    right_turn = (LANES - right_part) & (LANES - 1)
    right_pick = (lane < right_part + jnp.where(shift == 0, LANES, 0)) & (shift >= -LANES)
    is_left = [lane + i * LANES < drift_prev for i in range(WIN)]
    is_right = [lane + i * LANES >= HALF + drift_next for i in range(WIN)]

    def aligned(get, x, y):
        lines = [get(x, y, base + i) for i in range(OWN + 1)]
        return [pltpu.roll(jnp.where(stay, lines[i], lines[i + 1]), turn, 1) for i in range(OWN)]

    def windows(unit):
        low, high = got[0, unit, 0], got[0, unit, 1]
        a = [pltpu.roll(jnp.where(left_pick, low, high), left_turn, 1), pltpu.roll(high, left_turn, 1)]
        low, high = got[1, unit, 0], got[1, unit, 1]
        b = [pltpu.roll(low, right_turn, 1), pltpu.roll(jnp.where(right_pick, high, low), right_turn, 1)]
        return a, b

    def merged(get, x, y, unit):
        lines = aligned(get, x, y)
        a, b = windows(unit)
        for i in range(WIN):
            lines[i] = jnp.where(is_left[i], a[i], lines[i])
            lines[OWN - WIN + i] = jnp.where(is_right[i], b[i], lines[OWN - WIN + i])
        return lines

    def face(b, p):
        src, dst = ((face0, near0), (face1, near1))[b]
        return pltpu.make_async_remote_copy(
            src_ref=src.at[p], dst_ref=dst.at[1 - p], send_sem=face_send.at[2 * b + p],
            recv_sem=face_recv.at[2 * b + p], device_id=sides[2 + p][1], device_id_type=MESH,
        )

    def edge(side, p):
        return pltpu.make_async_remote_copy(
            src_ref=edge_out.at[side, p], dst_ref=edge_in.at[1 - side, p], send_sem=edge_send.at[2 * side + p],
            recv_sem=edge_recv.at[2 * side + p], device_id=sides[side][1], device_id_type=MESH,
        )

    for p in range(2):
        arrived(p)
        @pl.when(theres[p])
        def _():
            @pl.loop(0, SIDE // 2)
            def _(half):
                for x in (2 * half, 2 * half + 1):
                    lines = merged(field_of, x, outer[p], FIELD + p * SIDE + x)
                    for i in range(OWN):
                        face0[p, x, i] = lines[i]
            face(0, p).start()
    for p in range(2):
        arrived(2 + p)
        @pl.when(theres[p])
        def _():
            @pl.loop(0, SIDE)
            def _(x):
                for k, y in enumerate((outer[p], inner[p])):
                    lines = merged(inverse_of, x, y, FACTOR + (2 * p + k) * SIDE + x)
                    for i in range(OWN):
                        inv[p, k, x, i] = lines[i]

        @pl.when(jnp.logical_not(theres[p]))
        def _():
            @pl.loop(0, SIDE)
            def _(x):
                for k in range(2):
                    for i in range(OWN):
                        change[p, k, x, i] = jnp.zeros((SIDE, LANES), jnp.float32)
    for p in range(2):
        @pl.when(theres[p])
        def _():
            face(0, 1 - p).wait_recv()
            @pl.loop(0, SIDE)
            def _(x):
                for i in range(OWN):
                    value = near0[p, x, i] * inv[p, 0, x, i]
                    fix[p, x + 1, i] = value
                    change[p, 1, x, i] = value * inv[p, 1, x, i]
            turned = [pltpu.roll(fix[p, 1, i], LANES - 1, 1) for i in range(OWN)]
            edge_out[0, p] = turned[0]
            for i in range(OWN):
                fix[p, SIDE + 1, i] = jnp.where(lane == LANES - 1, turned[i + 1], turned[i]) if i + 1 < OWN else turned[i]
            turned = [pltpu.roll(fix[p, SIDE, i], 1, 1) for i in range(OWN)]
            edge_out[1, p] = turned[OWN - 1]
            for i in range(OWN):
                fix[p, 0, i] = jnp.where(lane == 0, turned[i - 1], turned[i]) if i else turned[i]
            for side in range(2):
                @pl.when(sides[side][0])
                def _():
                    edge(side, p).start()
    for p in range(2):
        arrived(4 + p)
        @pl.when(theres[p])
        def _():
            @pl.loop(0, SIDE // 2)
            def _(half):
                for x in (2 * half, 2 * half + 1):
                    lines = merged(first_of, x, outer[p], MIDDLE + p * SIDE + x)
                    for i in range(OWN):
                        face1[p, x, i] = lines[i] + fix[p, x + 1, i]
            face(1, p).start()
    for p in range(2):
        @pl.when(theres[p])
        def _():
            for side, x, i, spot in ((0, 0, 0, 0), (1, SIDE + 1, OWN - 1, LANES - 1)):
                @pl.when(sides[side][0])
                def _():
                    edge(1 - side, p).wait_recv()
                value = jnp.where(sides[side][0], edge_in[side, p], 0.0)
                fix[p, x, i] = jnp.where(lane == spot, value, fix[p, x, i])
            face(1, 1 - p).wait_recv()
            @pl.loop(0, SIDE)
            def _(x):
                for i in range(OWN):
                    total = near1[p, x, i] + (fix[p, x, i] + fix[p, x + 2, i]) + sums(fix[p, x + 1, i])
                    change[p, 0, x, i] = total * inv[p, 0, x, i]

    def at(x, y, i):
        return pl.ds((x * SIDE + y) * (SIDE * OWN) + i, SIDE, stride=OWN)

    spots = {0: (0, 0), 1: (0, 1), SIDE - 2: (1, 1), SIDE - 1: (1, 0)}
    window = [i for i in range(OWN) if i < WIN or i >= OWN - WIN]

    @pl.loop(0, SIDE)
    def _(x):
        for y in range(SIDE):
            lines = aligned(second_of, x, y)
            for i in range(OWN):
                if i in window:
                    kept[x, y, window.index(i)] = lines[i]
                elif y in spots:
                    out[at(x, y, i), :] = lines[i] + change[spots[y][0], spots[y][1], x, i]
                else:
                    out[at(x, y, i), :] = lines[i]
    for x in range(SIDE):
        arrived(6 + x)
        for y in range(SIDE):
            a, b = windows(FINAL + x * SIDE + y)
            for j, i in enumerate(window):
                value = jnp.where(is_left[i], a[i], kept[x, y, j]) if i < WIN else jnp.where(
                    is_right[j - WIN], b[j - WIN], kept[x, y, j]
                )
                if y in spots:
                    value = value + change[spots[y][0], spots[y][1], x, i]
                out[at(x, y, i), :] = value
    for side in range(2):
        @pl.when(sides[side][0])
        def _():
            greeted(side).wait_send()
    for p in range(2):
        @pl.when(theres[p])
        def _():
            for b in range(2):
                face(b, p).wait_send()
            for side in range(2):
                @pl.when(sides[side][0])
                def _():
                    edge(side, p).wait_send()
    for kind in range(KINDS):
        for side in range(2):
            @pl.when(needed(kind, side))
            def _():
                sent(kind, side).wait_send()


def local(state, coef, counts):
    n, groups = lax.axis_size("curve"), lax.axis_size("grp")
    cells, cap = state.shape[1], state.shape[3]
    rows = cap // LANES
    plane = SIDE * SIDE * rows
    f32 = jnp.float32
    vmem, hbm, smem = (pl.BlockSpec(memory_space=m) for m in (pltpu.VMEM, pltpu.HBM, pltpu.SMEM))
    tile = (SIDE, LANES)
    shapes = [(cells * rows + 2 * plane, LANES), (cells * rows, LANES), (cells * rows + PAD, LANES)]
    shapes += [(cells * rows + 2 * PAD, LANES), (cells * rows + 2 * plane, LANES), (cells * rows + 2 * PAD, LANES)]
    shapes += [(2, UNITS, WIN) + tile] * 2
    shapes += [(2, SIDE, OWN) + tile] * 4
    shapes += [(2, 2, SIDE, OWN) + tile, (2, SIDE + 2, OWN) + tile, (2, 2, SIDE, OWN) + tile]
    shapes += [(SIDE, SIDE, 2 * WIN) + tile] + [(2, 2) + tile] * 2
    out = pl.pallas_call(
        functools.partial(exchange, n, groups, rows),
        out_shape=jax.ShapeDtypeStruct((cells * OWN, LANES), f32),
        in_specs=[smem, hbm, hbm],
        out_specs=vmem,
        scratch_shapes=[
            pltpu.VMEM((1, LANES), jnp.int32),
            pltpu.VMEM((n, 1, LANES), jnp.int32),
            pltpu.SMEM((n, 1, LANES), jnp.int32),
            pltpu.VMEM((2,) + tile, f32),
            pltpu.VMEM((2,) + tile, f32),
        ]
        + [pltpu.VMEM(shape, f32) for shape in shapes]
        + [pltpu.SemaphoreType.DMA((k,)) for k in (n, n, 2, 2, 2, 3, 2 * KINDS, 2 * KINDS, 4, 4, 4, 4)],
        compiler_params=pltpu.CompilerParams(
            collective_id=0, has_side_effects=True, vmem_limit_bytes=48 * 1024 * 1024
        ),
    )(
        counts, state.reshape(2, cells * rows, LANES), coef.reshape(cells * rows, LANES),
    )
    return out.reshape(cells, 1, AVG)


def solution(mesh):
    placed = (P(None, None, "grp", "curve"), P(None, "grp", "curve"), P("grp", "curve"))
    return jax.shard_map(
        local, mesh=mesh, in_specs=placed, out_specs=P(None, "grp", "curve"), check_vma=False
    )
```

time: 66.4 us -> 52.6 us (0.79)
  Pallas kernels: 61.5 us -> 48.4 us
    pallas_call x1, Pallas kernels: 61.5 us -> 48.4 us  [local(): pl.pallas_call(functools.partial(exchange, n, groups, rows), out_shape=ja...]
where the time goes in v1:
time: 52.6 us; the launch traced here: 52.2 us
  Pallas kernels  48.4 us (92%)
  local copies, waits for them, and re-layouts  3.2 us (6%)
  between operations  0.67 us (1%)
    pallas_call x1, Pallas kernels, local(): pl.pallas_call(functools.partial(exchange, n, groups, rows), out_shape=ja...  48.4 us
    unnamed x3, local copies, waits for them, and re-layouts  3.2 us

profile of v1, /device:TPU:12, one launch (start us, length us, event | category | flops | bytes accessed | tf_op | source)
XLA Modules:
  0.0 52.2 jit_solution(15519781095749518338)
XLA Ops:
  0.7 0.0 copy-start
  0.7 1.9 %copy-done = f32[512,1,1536]{2,1,0:T(1,128)S(1)} copy-done((f32[512,1,1536]{2,1,0:T(1,128)S(1)}, f32[512,1,1536]{2,1,0:T(1,128)}, u32[]{:S(2)}) %copy-start) | copy-done | bytes 3145752
  2.5 48.4 %shard_map.37 = f32[4096,128]{1,0:T(8,128)S(1)} custom-call(s32[1,1]{1,0:T(1,128)S(6)} %copy.6.counts, f32[2,6144,128]{2,1,0:T(8,128)} %bitcast.5, f32[6144,128]{1,0:T(8,128)S(1)} %bitcast.4), custom_call_target="tpu_custom_call" | custom-call | tf_op jit(solution)/shard_map/pallas_call | solution.py:459
  50.9 1.3 %copy.7 = f32[512,1,1024]{2,1,0:T(1,128)} copy(f32[512,1,1024]{2,1,0:T(1,128)S(1)} %bitcast.3) | data formatting | bytes 4194304
Async XLA Ops:
  0.7 1.9 %copy-start = (f32[512,1,1536]{2,1,0:T(1,128)S(1)}, f32[512,1,1536]{2,1,0:T(1,128)}, u32[]{:S(2)}) copy-start(f32[512,1,1536]{2,1,0:T(1,128)} %param.4) | copy-start | bytes 9437188

commit v2 on v1

--- a/solution.py
+++ b/solution.py
@@ -18,6 +18,7 @@
 UNITS = 16 * SIDE
 KINDS = 6 + SIDE
 MESH = pl.DeviceIdType.MESH
+EARLY_ACROSS, EARLY_PAIRED = 4, 3
 
 
 def exchange(
@@ -107,9 +108,11 @@
     def needed(kind, side):
         return sides[side][0] & theres[kind % 2] if kind < 6 else sides[side][0]
 
-    def send(kind):
+    paired = lax.rem(rank, 2) == 1, lax.rem(rank, 2) == 0
+
+    def send(kind, only=(True, True)):
         for side in range(2):
-            @pl.when(needed(kind, side))
+            @pl.when(needed(kind, side) & only[side])
             def _():
                 sent(kind, side).start()
 
@@ -119,18 +122,20 @@
             def _():
                 sent(kind, 1 - side).wait_recv()
 
+    def spread(step, fn):
+        @pl.loop(0, SIDE // step)
+        def _(part):
+            for at in range(step):
+                fn(step * part + at)
+
     outer, inner = (0, SIDE - 1), (1, SIDE - 2)
     loads[0].wait()
-    @pl.loop(0, SIDE)
-    def _(x):
+
+    def step(x):
         for p in range(2):
             pack(FIELD + p * SIDE + x, field_of, x, outer[p])
+    spread(4, step)
     loads[2].wait()
-    @pl.loop(0, SIDE)
-    def _(x):
-        for p in range(2):
-            for k, y in enumerate((outer[p], inner[p])):
-                pack(FACTOR + (2 * p + k) * SIDE + x, factor_of, x, y)
     loads[1].wait()
     for side, at, turn, outer_x, near_x in ((0, 0, 0, 1, 0), (1, last_row, LANES - last_lane, SIDE - 2, SIDE - 1)):
         packed = jnp.zeros((SIDE, LANES), jnp.float32)
@@ -166,7 +171,15 @@
         tallies[-1].start()
     keep = pltpu.make_async_copy(mine, every.at[rank], local_sem.at[0])
     keep.start()
-    for kind in range(4):
+    for kind in range(2):
+        send(kind)
+
+    def step(x):
+        for p in range(2):
+            for k, y in enumerate((outer[p], inner[p])):
+                pack(FACTOR + (2 * p + k) * SIDE + x, factor_of, x, y)
+    spread(4, step)
+    for kind in range(2, 4):
         send(kind)
 
     for side in range(2):
@@ -181,9 +194,8 @@
         return above + jnp.where(level > 0, pltpu.roll(value, 1, 0), 0.0)
 
     def borders(get, store, ghosts, spot):
-        @pl.loop(0, SIDE // 2)
-        def _(half):
-            for y in (2 * half, 2 * half + 1):
+        def step(y):
+            if True:
                 turned = [pltpu.roll(get(SIDE - 1, y, r), 1, 1) for r in range(rows)]
                 carry = pltpu.roll(ghosts[0], (LANES - spot - y) & (LANES - 1), 1)
                 for r in range(rows):
@@ -194,6 +206,7 @@
                 for r in range(rows):
                     value = jnp.where(lane == LANES - 1, turned[r + 1], turned[r]) if r + 1 < rows else turned[r]
                     store(SIDE, y, r, jnp.where(lane + r * LANES == last, ghost, value))
+        spread(4, step)
 
     def sweep(get, factor, store):
         @pl.loop(0, SIDE)
@@ -233,10 +246,11 @@
 
     borders(field_of, store_field, seen, SIDE)
     sweep(field_of, made_factor, store_first)
-    @pl.loop(0, SIDE)
-    def _(x):
+
+    def step(x):
         for p in range(2):
             pack(MIDDLE + p * SIDE + x, first_of, x, outer[p])
+    spread(4, step)
     for kind in range(4, 6):
         send(kind)
 
@@ -251,12 +265,16 @@
     seen = [moved(seen[side], shown[side]) for side in range(2)]
     borders(first_of, store_first, seen, 0)
     sweep(first_of, inverse_of, store_second)
-    @pl.loop(0, SIDE)
-    def _(x):
+
+    def step(x):
         for y in range(SIDE):
             pack(FINAL + x * SIDE + y, second_of, x, y)
+    spread(2, step)
+    across = [jnp.logical_not(x) for x in paired]
     for kind in range(6, KINDS):
-        send(kind)
+        for only, count in ((across, EARLY_ACROSS), (paired, EARLY_PAIRED)):
+            if kind - 6 < count:
+                send(kind, only)
 
     keep.wait()
     for copy in tallies:
@@ -320,23 +338,22 @@
         arrived(p)
         @pl.when(theres[p])
         def _():
-            @pl.loop(0, SIDE // 2)
-            def _(half):
-                for x in (2 * half, 2 * half + 1):
-                    lines = merged(field_of, x, outer[p], FIELD + p * SIDE + x)
-                    for i in range(OWN):
-                        face0[p, x, i] = lines[i]
+            def step(x):
+                lines = merged(field_of, x, outer[p], FIELD + p * SIDE + x)
+                for i in range(OWN):
+                    face0[p, x, i] = lines[i]
+            spread(4, step)
             face(0, p).start()
     for p in range(2):
         arrived(2 + p)
         @pl.when(theres[p])
         def _():
-            @pl.loop(0, SIDE)
-            def _(x):
+            def step(x):
                 for k, y in enumerate((outer[p], inner[p])):
                     lines = merged(inverse_of, x, y, FACTOR + (2 * p + k) * SIDE + x)
                     for i in range(OWN):
                         inv[p, k, x, i] = lines[i]
+            spread(4, step)
 
         @pl.when(jnp.logical_not(theres[p]))
         def _():
@@ -358,11 +375,11 @@
             turned = [pltpu.roll(fix[p, 1, i], LANES - 1, 1) for i in range(OWN)]
             edge_out[0, p] = turned[0]
             for i in range(OWN):
-                fix[p, SIDE + 1, i] = jnp.where(lane == LANES - 1, turned[i + 1], turned[i]) if i + 1 < OWN else turned[i]
+                fix[p, SIDE + 1, i] = jnp.where(lane == LANES - 1, turned[i + 1] if i + 1 < OWN else 0.0, turned[i])
             turned = [pltpu.roll(fix[p, SIDE, i], 1, 1) for i in range(OWN)]
             edge_out[1, p] = turned[OWN - 1]
             for i in range(OWN):
-                fix[p, 0, i] = jnp.where(lane == 0, turned[i - 1], turned[i]) if i else turned[i]
+                fix[p, 0, i] = jnp.where(lane == 0, turned[i - 1] if i else 0.0, turned[i])
             for side in range(2):
                 @pl.when(sides[side][0])
                 def _():
@@ -371,22 +388,19 @@
         arrived(4 + p)
         @pl.when(theres[p])
         def _():
-            @pl.loop(0, SIDE // 2)
-            def _(half):
-                for x in (2 * half, 2 * half + 1):
-                    lines = merged(first_of, x, outer[p], MIDDLE + p * SIDE + x)
-                    for i in range(OWN):
-                        face1[p, x, i] = lines[i] + fix[p, x + 1, i]
+            def step(x):
+                lines = merged(first_of, x, outer[p], MIDDLE + p * SIDE + x)
+                for i in range(OWN):
+                    face1[p, x, i] = lines[i] + fix[p, x + 1, i]
+            spread(4, step)
             face(1, p).start()
+    for kind in range(6, KINDS):
+        for only, count in ((across, EARLY_ACROSS), (paired, EARLY_PAIRED)):
+            if kind - 6 >= count:
+                send(kind, only)
     for p in range(2):
         @pl.when(theres[p])
         def _():
-            for side, x, i, spot in ((0, 0, 0, 0), (1, SIDE + 1, OWN - 1, LANES - 1)):
-                @pl.when(sides[side][0])
-                def _():
-                    edge(1 - side, p).wait_recv()
-                value = jnp.where(sides[side][0], edge_in[side, p], 0.0)
-                fix[p, x, i] = jnp.where(lane == spot, value, fix[p, x, i])
             face(1, 1 - p).wait_recv()
             @pl.loop(0, SIDE)
             def _(x):
@@ -411,6 +425,13 @@
                     out[at(x, y, i), :] = lines[i] + change[spots[y][0], spots[y][1], x, i]
                 else:
                     out[at(x, y, i), :] = lines[i]
+    for p in range(2):
+        for side, x, i, spot in ((0, 0, 0, 0), (1, SIDE - 1, OWN - 1, LANES - 1)):
+            @pl.when(theres[p] & sides[side][0])
+            def _():
+                edge(1 - side, p).wait_recv()
+                value = jnp.where(lane == spot, edge_in[side, p] * inv[p, 0, x, i], 0.0)
+                change[p, 0, x, i] = change[p, 0, x, i] + value
     for x in range(SIDE):
         arrived(6 + x)
         for y in range(SIDE):
@@ -471,7 +492,7 @@
         + [pltpu.VMEM(shape, f32) for shape in shapes]
         + [pltpu.SemaphoreType.DMA((k,)) for k in (n, n, 2, 2, 2, 3, 2 * KINDS, 2 * KINDS, 4, 4, 4, 4)],
         compiler_params=pltpu.CompilerParams(
-            collective_id=0, has_side_effects=True, vmem_limit_bytes=48 * 1024 * 1024
+            collective_id=0, has_side_effects=True, vmem_limit_bytes=50 * 1024 * 1024
         ),
     )(
         counts, state.reshape(2, cells * rows, LANES), coef.reshape(cells * rows, LANES),

time: 52.6 us -> 49.1 us (0.933)
  local copies, waits for them, and re-layouts: 3.2 us -> 1.32 us
  Pallas kernels: 48.4 us -> 46.9 us
    unnamed x3 -> x1, local copies, waits for them, and re-layouts: 3.2 us -> 1.32 us
    pallas_call x1, Pallas kernels: 48.4 us -> 46.9 us  [local(): pl.pallas_call(functools.partial(exchange, n, groups, rows), out_shape=ja...]
where the time goes in v2:
time: 49.1 us; the launch traced here: 48.8 us
  Pallas kernels  46.9 us (96%)
  local copies, waits for them, and re-layouts  1.32 us (3%)
  between operations  0.66 us (1%)
    pallas_call x1, Pallas kernels, local(): pl.pallas_call(functools.partial(exchange, n, groups, rows), out_shape=ja...  46.9 us
    unnamed x1, local copies, waits for them, and re-layouts  1.32 us

profile of v2, /device:TPU:12, one launch (start us, length us, event | category | flops | bytes accessed | tf_op | source)
XLA Modules:
  0.0 48.8 jit_solution(4417933430840657255)
XLA Ops:
  0.7 46.9 %shard_map.37 = f32[4096,128]{1,0:T(8,128)S(1)} custom-call(s32[1,1]{1,0:T(1,128)S(6)} %copy.6.counts, f32[2,6144,128]{2,1,0:T(8,128)} %bitcast.4, f32[6144,128]{1,0:T(8,128)} %bitcast.5), custom_call_target="tpu_custom_call" | custom-call | tf_op jit(solution)/shard_map/pallas_call | solution.py:480
  47.5 1.3 %copy.7 = f32[512,1,1024]{2,1,0:T(1,128)} copy(f32[512,1,1024]{2,1,0:T(1,128)S(1)} %bitcast.3) | data formatting | bytes 4194304

commit v3 on v2

--- a/solution.py
+++ b/solution.py
@@ -16,15 +16,16 @@
 PAD = 16
 FIELD, FACTOR, MIDDLE, FINAL = 0, 2 * SIDE, 6 * SIDE, 8 * SIDE
 UNITS = 16 * SIDE
-KINDS = 6 + SIDE
+KINDS = 8 + SIDE
 MESH = pl.DeviceIdType.MESH
-EARLY_ACROSS, EARLY_PAIRED = 4, 3
+EARLY = 3
 
 
 def exchange(
     n, groups, rows, counts, state, coef, out, mine, every, every_s, ends, met, raw0, raw1, raw2, inverse, first,
     second, put, got, face0, face1, near0, near1, inv, fix, change, kept, edge_out, edge_in, count_send, count_recv,
     end_send, end_recv, local_sem, load_sem, send_sem, recv_sem, face_send, face_recv, edge_send, edge_recv,
+    via_end, via_end_send, via_end_recv, via, via_send, via_recv,
 ):
     plane_rows = SIDE * SIDE * rows
     cells_rows = SIDE * plane_rows
@@ -92,10 +93,12 @@
         if kind < 2:
             return FIELD + kind * SIDE, SIDE
         if kind < 4:
-            return FACTOR + (kind - 2) * 2 * SIDE, 2 * SIDE
+            return FACTOR + (kind - 2) * SIDE, SIDE
         if kind < 6:
             return MIDDLE + (kind - 4) * SIDE, SIDE
-        return FINAL + (kind - 6) * SIDE, SIDE
+        if kind < 8:
+            return FACTOR + (kind - 4) * SIDE, SIDE
+        return FINAL + (kind - 8) * SIDE, SIDE
 
     def sent(kind, side):
         start, count = message(kind)
@@ -106,9 +109,38 @@
         )
 
     def needed(kind, side):
-        return sides[side][0] & theres[kind % 2] if kind < 6 else sides[side][0]
+        return sides[side][0] & theres[kind % 2] if kind < 8 else sides[side][0]
 
     paired = lax.rem(rank, 2) == 1, lax.rem(rank, 2) == 0
+    across = [jnp.logical_not(x) for x in paired]
+    passes = paired[0] & (rank >= 2), paired[1] & (rank < n - 2)
+    beyond = {"curve": rank - 2}, {"curve": rank + 2}
+    steps = max(n // 2 - 1, 1)
+
+    def routed(side, owner):
+        return (owner if side == 0 else n - 1 - owner) // 2 * SIDE // steps
+
+    def lent(c, side):
+        start, count = message(8 + c)
+        return pltpu.make_async_remote_copy(
+            src_ref=put.at[side, pl.ds(start, count)], dst_ref=via.at[c],
+            send_sem=send_sem.at[side * KINDS + 8 + c], recv_sem=via_recv.at[c],
+            device_id=sides[1 - side][1], device_id_type=MESH,
+        )
+
+    def passed(c, side):
+        start, count = message(8 + c)
+        return pltpu.make_async_remote_copy(
+            src_ref=via.at[c], dst_ref=got.at[1 - side, pl.ds(start, count)],
+            send_sem=via_send.at[c], recv_sem=recv_sem.at[side * KINDS + 8 + c],
+            device_id=beyond[side], device_id_type=MESH,
+        )
+
+    def lending(c, side):
+        return sides[side][0] & across[side] & (c < routed(side, rank))
+
+    def passing(c, side):
+        return passes[side] & (c < routed(side, rank - 1 + 2 * side))
 
     def send(kind, only=(True, True)):
         for side in range(2):
@@ -155,8 +187,24 @@
             recv_sem=end_recv.at[side], device_id=sides[side][1], device_id_type=MESH,
         )
 
+    def greeted_via(side):
+        return pltpu.make_async_remote_copy(
+            src_ref=ends.at[side], dst_ref=via_end, send_sem=end_send.at[side],
+            recv_sem=via_end_recv, device_id=sides[1 - side][1], device_id_type=MESH,
+        )
+
+    def greeted_on(side):
+        return pltpu.make_async_remote_copy(
+            src_ref=via_end, dst_ref=met.at[1 - side], send_sem=via_end_send,
+            recv_sem=end_recv.at[side], device_id=beyond[side], device_id_type=MESH,
+        )
+
     for side in range(2):
-        @pl.when(sides[side][0])
+        @pl.when(sides[side][0] & across[side])
+        def _():
+            greeted_via(side).start()
+    for side in range(2):
+        @pl.when(sides[side][0] & paired[side])
         def _():
             greeted(side).start()
     tallies = []
@@ -177,11 +225,16 @@
     def step(x):
         for p in range(2):
             for k, y in enumerate((outer[p], inner[p])):
-                pack(FACTOR + (2 * p + k) * SIDE + x, factor_of, x, y)
+                pack(FACTOR + (2 * k + p) * SIDE + x, factor_of, x, y)
     spread(4, step)
     for kind in range(2, 4):
         send(kind)
 
+    for side in range(2):
+        @pl.when(passes[side])
+        def _():
+            greeted_via(side).wait_recv()
+            greeted_on(side).start()
     for side in range(2):
         @pl.when(sides[side][0])
         def _():
@@ -251,7 +304,7 @@
         for p in range(2):
             pack(MIDDLE + p * SIDE + x, first_of, x, outer[p])
     spread(4, step)
-    for kind in range(4, 6):
+    for kind in range(4, 8):
         send(kind)
 
     def moved(met_end, own_end):
@@ -270,12 +323,19 @@
         for y in range(SIDE):
             pack(FINAL + x * SIDE + y, second_of, x, y)
     spread(2, step)
-    across = [jnp.logical_not(x) for x in paired]
-    for kind in range(6, KINDS):
-        for only, count in ((across, EARLY_ACROSS), (paired, EARLY_PAIRED)):
-            if kind - 6 < count:
-                send(kind, only)
-
+    for c in range(SIDE):
+        for side in range(2):
+            @pl.when(lending(c, side))
+            def _():
+                lent(c, side).start()
+
+    def release(early):
+        for c in range(SIDE):
+            for side in range(2):
+                @pl.when(sides[side][0] & jnp.where(across[side], (c >= routed(side, rank)) & early, early == (c < EARLY)))
+                def _():
+                    sent(8 + c, side).start()
+    release(True)
     keep.wait()
     for copy in tallies:
         copy.wait()
@@ -349,10 +409,9 @@
         @pl.when(theres[p])
         def _():
             def step(x):
-                for k, y in enumerate((outer[p], inner[p])):
-                    lines = merged(inverse_of, x, y, FACTOR + (2 * p + k) * SIDE + x)
-                    for i in range(OWN):
-                        inv[p, k, x, i] = lines[i]
+                lines = merged(inverse_of, x, outer[p], FACTOR + p * SIDE + x)
+                for i in range(OWN):
+                    inv[p, x, i] = lines[i]
             spread(4, step)
 
         @pl.when(jnp.logical_not(theres[p]))
@@ -369,9 +428,8 @@
             @pl.loop(0, SIDE)
             def _(x):
                 for i in range(OWN):
-                    value = near0[p, x, i] * inv[p, 0, x, i]
+                    value = near0[p, x, i] * inv[p, x, i]
                     fix[p, x + 1, i] = value
-                    change[p, 1, x, i] = value * inv[p, 1, x, i]
             turned = [pltpu.roll(fix[p, 1, i], LANES - 1, 1) for i in range(OWN)]
             edge_out[0, p] = turned[0]
             for i in range(OWN):
@@ -394,10 +452,7 @@
                     face1[p, x, i] = lines[i] + fix[p, x + 1, i]
             spread(4, step)
             face(1, p).start()
-    for kind in range(6, KINDS):
-        for only, count in ((across, EARLY_ACROSS), (paired, EARLY_PAIRED)):
-            if kind - 6 >= count:
-                send(kind, only)
+    release(False)
     for p in range(2):
         @pl.when(theres[p])
         def _():
@@ -406,7 +461,22 @@
             def _(x):
                 for i in range(OWN):
                     total = near1[p, x, i] + (fix[p, x, i] + fix[p, x + 2, i]) + sums(fix[p, x + 1, i])
-                    change[p, 0, x, i] = total * inv[p, 0, x, i]
+                    change[p, 0, x, i] = total * inv[p, x, i]
+    for p in range(2):
+        arrived(6 + p)
+        @pl.when(theres[p])
+        def _():
+            def step(x):
+                lines = merged(inverse_of, x, inner[p], FACTOR + (2 + p) * SIDE + x)
+                for i in range(OWN):
+                    change[p, 1, x, i] = lines[i] * fix[p, x + 1, i]
+            spread(4, step)
+    for c in range(SIDE):
+        for side in range(2):
+            @pl.when(passing(c, side))
+            def _():
+                lent(c, side).wait_recv()
+                passed(c, side).start()
 
     def at(x, y, i):
         return pl.ds((x * SIDE + y) * (SIDE * OWN) + i, SIDE, stride=OWN)
@@ -425,15 +495,19 @@
                     out[at(x, y, i), :] = lines[i] + change[spots[y][0], spots[y][1], x, i]
                 else:
                     out[at(x, y, i), :] = lines[i]
-    for p in range(2):
-        for side, x, i, spot in ((0, 0, 0, 0), (1, SIDE - 1, OWN - 1, LANES - 1)):
-            @pl.when(theres[p] & sides[side][0])
-            def _():
-                edge(1 - side, p).wait_recv()
-                value = jnp.where(lane == spot, edge_in[side, p] * inv[p, 0, x, i], 0.0)
-                change[p, 0, x, i] = change[p, 0, x, i] + value
-    for x in range(SIDE):
-        arrived(6 + x)
+    def settle():
+        for p in range(2):
+            for side, x, i, spot in ((0, 0, 0, 0), (1, SIDE - 1, OWN - 1, LANES - 1)):
+                @pl.when(theres[p] & sides[side][0])
+                def _():
+                    edge(1 - side, p).wait_recv()
+                    value = jnp.where(lane == spot, edge_in[side, p] * inv[p, x, i], 0.0)
+                    change[p, 0, x, i] = change[p, 0, x, i] + value
+
+    for x in (1, 2, 3, 4, 5, 6, 0, 7):
+        if x == 0:
+            settle()
+        arrived(8 + x)
         for y in range(SIDE):
             a, b = windows(FINAL + x * SIDE + y)
             for j, i in enumerate(window):
@@ -444,6 +518,15 @@
                     value = value + change[spots[y][0], spots[y][1], x, i]
                 out[at(x, y, i), :] = value
     for side in range(2):
+        @pl.when(passes[side])
+        def _():
+            greeted_on(side).wait_send()
+
+        for c in range(SIDE):
+            @pl.when(passing(c, side))
+            def _():
+                passed(c, side).wait_send()
+
         @pl.when(sides[side][0])
         def _():
             greeted(side).wait_send()
@@ -475,7 +558,7 @@
     shapes += [(cells * rows + 2 * PAD, LANES), (cells * rows + 2 * plane, LANES), (cells * rows + 2 * PAD, LANES)]
     shapes += [(2, UNITS, WIN) + tile] * 2
     shapes += [(2, SIDE, OWN) + tile] * 4
-    shapes += [(2, 2, SIDE, OWN) + tile, (2, SIDE + 2, OWN) + tile, (2, 2, SIDE, OWN) + tile]
+    shapes += [(2, SIDE, OWN) + tile, (2, SIDE + 2, OWN) + tile, (2, 2, SIDE, OWN) + tile]
     shapes += [(SIDE, SIDE, 2 * WIN) + tile] + [(2, 2) + tile] * 2
     out = pl.pallas_call(
         functools.partial(exchange, n, groups, rows),
@@ -490,7 +573,9 @@
             pltpu.VMEM((2,) + tile, f32),
         ]
         + [pltpu.VMEM(shape, f32) for shape in shapes]
-        + [pltpu.SemaphoreType.DMA((k,)) for k in (n, n, 2, 2, 2, 3, 2 * KINDS, 2 * KINDS, 4, 4, 4, 4)],
+        + [pltpu.SemaphoreType.DMA((k,)) for k in (n, n, 2, 2, 2, 3, 2 * KINDS, 2 * KINDS, 4, 4, 4, 4)]
+        + [pltpu.VMEM(tile, f32)] + [pltpu.SemaphoreType.DMA] * 2
+        + [pltpu.VMEM((SIDE, SIDE, WIN) + tile, f32)] + [pltpu.SemaphoreType.DMA((SIDE,))] * 2,
         compiler_params=pltpu.CompilerParams(
             collective_id=0, has_side_effects=True, vmem_limit_bytes=50 * 1024 * 1024
         ),

time: 49.1 us -> 46.4 us (0.945)
  the two profiles are of different devices: /device:TPU:12 before, /device:TPU:28 now
where the time goes in v3:
time: 46.4 us; the launch traced here: 46.2 us
  Pallas kernels  44.3 us (95%)
  local copies, waits for them, and re-layouts  1.32 us (3%)
  between operations  0.66 us (1%)
    pallas_call x1, Pallas kernels, local(): pl.pallas_call(functools.partial(exchange, n, groups, rows), out_shape=ja...  44.3 us
    unnamed x1, local copies, waits for them, and re-layouts  1.32 us

profile of v3, /device:TPU:28, one launch (start us, length us, event | category | flops | bytes accessed | tf_op | source)
XLA Modules:
  0.0 46.2 jit_solution(16284858732123842752)
XLA Ops:
  0.7 44.3 %shard_map.37 = f32[4096,128]{1,0:T(8,128)S(1)} custom-call(s32[1,1]{1,0:T(1,128)S(6)} %copy.6.counts, f32[2,6144,128]{2,1,0:T(8,128)} %bitcast.4, f32[6144,128]{1,0:T(8,128)} %bitcast.5), custom_call_target="tpu_custom_call" | custom-call | tf_op jit(solution)/shard_map/pallas_call | solution.py:563
  44.9 1.3 %copy.7 = f32[512,1,1024]{2,1,0:T(1,128)} copy(f32[512,1,1024]{2,1,0:T(1,128)S(1)} %bitcast.3) | data formatting | bytes 4194304

commit v4 on v3

--- a/solution.py
+++ b/solution.py
@@ -26,6 +26,7 @@
     second, put, got, face0, face1, near0, near1, inv, fix, change, kept, edge_out, edge_in, count_send, count_recv,
     end_send, end_recv, local_sem, load_sem, send_sem, recv_sem, face_send, face_recv, edge_send, edge_recv,
     via_end, via_end_send, via_end_recv, via, via_send, via_recv,
+    rim,
 ):
     plane_rows = SIDE * SIDE * rows
     cells_rows = SIDE * plane_rows
@@ -39,9 +40,24 @@
     theres = (has_low, has_high)
     raw = (raw0, raw1, raw2)
     front = (plane_rows, 0, 0)
-    loads = {}
-    for f, src in ((0, state.at[0]), (2, coef), (1, state.at[1])):
-        loads[f] = pltpu.make_async_copy(src, raw[f].at[pl.ds(front[f], cells_rows)], load_sem.at[f])
+    band = SIDE * rows
+    for p, y in enumerate((0, SIDE - 1)):
+        for x in range(SIDE):
+            pltpu.make_async_copy(
+                state.at[0, pl.ds((x * SIDE + y) * band, band)], rim.at[pl.ds((p * SIDE + x) * band, band)], load_sem.at[3]
+            ).start()
+    sources = (state.at[0], state.at[1], coef)
+
+    def load(f, x, count, sem):
+        return pltpu.make_async_copy(
+            sources[f].at[pl.ds(x * plane_rows, count * plane_rows)],
+            raw[f].at[pl.ds(front[f] + x * plane_rows, count * plane_rows)], load_sem.at[sem],
+        )
+
+    for f, x, count in ((0, 0, 2), (0, SIDE - 2, 2), (1, 0, 1), (1, SIDE - 1, 1), (2, 0, 1), (2, SIDE - 1, 1)):
+        load(f, x, count, 4).start()
+    loads = {0: load(0, 2, SIDE - 4, 0), 2: load(2, 1, SIDE - 2, 2), 1: load(1, 1, SIDE - 2, 1)}
+    for f in (2, 0, 1):
         loads[f].start()
     barrier = pltpu.get_barrier_semaphore()
     for there, device in sides:
@@ -104,8 +120,15 @@
         start, count = message(kind)
         return pltpu.make_async_remote_copy(
             src_ref=put.at[side, pl.ds(start, count)], dst_ref=got.at[1 - side, pl.ds(start, count)],
-            send_sem=send_sem.at[side * KINDS + kind], recv_sem=recv_sem.at[side * KINDS + kind],
+            send_sem=send_sem.at[3 * side + (kind % 2 if kind < 8 else 2)], recv_sem=recv_sem.at[side * KINDS + kind],
             device_id=sides[side][1], device_id_type=MESH,
+        )
+
+    def leaving(side, group):
+        units = pl.ds(FINAL, SIDE * SIDE) if group == 2 else pl.ds(0, 4 * SIDE)
+        return pltpu.make_async_remote_copy(
+            src_ref=put.at[side, units], dst_ref=got.at[1 - side, units], send_sem=send_sem.at[3 * side + group],
+            recv_sem=recv_sem.at[side * KINDS], device_id=sides[side][1], device_id_type=MESH,
         )
 
     def needed(kind, side):
@@ -118,13 +141,13 @@
     steps = max(n // 2 - 1, 1)
 
     def routed(side, owner):
-        return (owner if side == 0 else n - 1 - owner) // 2 * SIDE // steps
+        return (owner if side == 0 else n - 1 - owner) // 2 * (SIDE + 1) // steps
 
     def lent(c, side):
         start, count = message(8 + c)
         return pltpu.make_async_remote_copy(
             src_ref=put.at[side, pl.ds(start, count)], dst_ref=via.at[c],
-            send_sem=send_sem.at[side * KINDS + 8 + c], recv_sem=via_recv.at[c],
+            send_sem=send_sem.at[3 * side + 2], recv_sem=via_recv.at[c],
             device_id=sides[1 - side][1], device_id_type=MESH,
         )
 
@@ -161,19 +184,32 @@
                 fn(step * part + at)
 
     outer, inner = (0, SIDE - 1), (1, SIDE - 2)
-    loads[0].wait()
+    pltpu.make_async_copy(
+        state.at[0, pl.ds(0, 2 * SIDE * band)], rim.at[pl.ds(0, 2 * SIDE * band)], load_sem.at[3]
+    ).wait()
+
+    def rim_of(x, p, r):
+        return rim[pl.ds((p * SIDE + x) * band + r, SIDE, stride=rows), :]
 
     def step(x):
         for p in range(2):
-            pack(FIELD + p * SIDE + x, field_of, x, outer[p])
+            pack(FIELD + p * SIDE + x, rim_of, x, p)
     spread(4, step)
-    loads[2].wait()
-    loads[1].wait()
-    for side, at, turn, outer_x, near_x in ((0, 0, 0, 1, 0), (1, last_row, LANES - last_lane, SIDE - 2, SIDE - 1)):
+    load(0, 0, SIDE, 4).wait()
+    picks = [jnp.zeros((SIDE, LANES), jnp.int32) + last_row == r for r in range(rows)]
+
+    def end_of(f, x, y, at):
+        value = raw[f][raw_at(f, x, y, at), :]
+        if at:
+            for r in range(2 * HALF // LANES - 1, at):
+                value = jnp.where(picks[r], raw[f][raw_at(f, x, y, r), :], value)
+        return 1.0 / (value + 6.0) if f == 2 else value
+
+    for side, at, turn, outer_x, near_x in ((0, 0, 0, 1, 0), (1, rows - 1, LANES - last_lane, SIDE - 2, SIDE - 1)):
         packed = jnp.zeros((SIDE, LANES), jnp.float32)
         for p, (f, x) in enumerate(((0, outer_x), (0, near_x), (1, near_x), (2, near_x))):
             for y in range(SIDE):
-                value = factor_of(x, y, at) if f == 2 else raw[f][raw_at(f, x, y, at), :]
+                value = end_of(f, x, y, at)
                 spot = p * SIDE + y
                 value = pltpu.roll(value, (turn + spot) & (LANES - 1), 1)
                 packed = jnp.where(lane == spot, value, packed)
@@ -207,20 +243,21 @@
         @pl.when(sides[side][0] & paired[side])
         def _():
             greeted(side).start()
-    tallies = []
     for off in range(1, n):
-        tallies.append(
-            pltpu.make_async_remote_copy(
-                src_ref=mine, dst_ref=every.at[rank], send_sem=count_send.at[off],
-                recv_sem=count_recv.at[off], device_id={"curve": lax.rem(rank + off, n)},
-                device_id_type=MESH,
-            )
-        )
-        tallies[-1].start()
+        pltpu.make_async_remote_copy(
+            src_ref=mine, dst_ref=every.at[rank], send_sem=count_send, recv_sem=count_recv,
+            device_id={"curve": lax.rem(rank + off, n)}, device_id_type=MESH,
+        ).start()
+    tallies = pltpu.make_async_remote_copy(
+        src_ref=every.at[pl.ds(0, n - 1)], dst_ref=every.at[pl.ds(0, n - 1)], send_sem=count_send,
+        recv_sem=count_recv, device_id={"curve": lax.rem(rank + 1, n)}, device_id_type=MESH,
+    )
     keep = pltpu.make_async_copy(mine, every.at[rank], local_sem.at[0])
     keep.start()
     for kind in range(2):
         send(kind)
+    for f in (2, 0, 1):
+        loads[f].wait()
 
     def step(x):
         for p in range(2):
@@ -329,16 +366,17 @@
             def _():
                 lent(c, side).start()
 
+    soon = jnp.where((rank == 1) | (rank == n - 2), SIDE, EARLY)
+
     def release(early):
         for c in range(SIDE):
             for side in range(2):
-                @pl.when(sides[side][0] & jnp.where(across[side], (c >= routed(side, rank)) & early, early == (c < EARLY)))
+                @pl.when(sides[side][0] & jnp.where(across[side], (c >= routed(side, rank)) & early, early == (c < soon)))
                 def _():
                     sent(8 + c, side).start()
     release(True)
     keep.wait()
-    for copy in tallies:
-        copy.wait()
+    tallies.wait()
     keep = pltpu.make_async_copy(every, every_s, local_sem.at[1])
     keep.start()
     keep.wait()
@@ -539,11 +577,11 @@
                 @pl.when(sides[side][0])
                 def _():
                     edge(side, p).wait_send()
-    for kind in range(KINDS):
-        for side in range(2):
-            @pl.when(needed(kind, side))
+    for side in range(2):
+        for group, there in enumerate((has_low, has_high, True)):
+            @pl.when(sides[side][0] & there)
             def _():
-                sent(kind, side).wait_send()
+                leaving(side, group).wait_send()
 
 
 def local(state, coef, counts):
@@ -573,9 +611,11 @@
             pltpu.VMEM((2,) + tile, f32),
         ]
         + [pltpu.VMEM(shape, f32) for shape in shapes]
-        + [pltpu.SemaphoreType.DMA((k,)) for k in (n, n, 2, 2, 2, 3, 2 * KINDS, 2 * KINDS, 4, 4, 4, 4)]
+        + [pltpu.SemaphoreType.DMA] * 2
+        + [pltpu.SemaphoreType.DMA((k,)) for k in (2, 2, 2, 5, 6, 2 * KINDS, 4, 4, 4, 4)]
         + [pltpu.VMEM(tile, f32)] + [pltpu.SemaphoreType.DMA] * 2
-        + [pltpu.VMEM((SIDE, SIDE, WIN) + tile, f32)] + [pltpu.SemaphoreType.DMA((SIDE,))] * 2,
+        + [pltpu.VMEM((SIDE, SIDE, WIN) + tile, f32)] + [pltpu.SemaphoreType.DMA((SIDE,))] * 2
+        + [pltpu.VMEM((2 * SIDE * SIDE * rows + PAD, LANES), f32)],
         compiler_params=pltpu.CompilerParams(
             collective_id=0, has_side_effects=True, vmem_limit_bytes=50 * 1024 * 1024
         ),

time: 46.4 us -> 44.9 us (0.968)
  the two profiles are of different devices: /device:TPU:28 before, /device:TPU:12 now
where the time goes in v4:
time: 44.9 us; the launch traced here: 44.6 us
  Pallas kernels  42.6 us (95%)
  local copies, waits for them, and re-layouts  1.32 us (3%)
  between operations  0.66 us (1%)
    pallas_call x1, Pallas kernels, local(): pl.pallas_call(functools.partial(exchange, n, groups, rows), out_shape=ja...  42.6 us
    unnamed x1, local copies, waits for them, and re-layouts  1.32 us

profile of v4, /device:TPU:12, one launch (start us, length us, event | category | flops | bytes accessed | tf_op | source)
XLA Modules:
  0.0 44.6 jit_solution(1491064509274943478)
XLA Ops:
  0.7 42.6 %shard_map.37 = f32[4096,128]{1,0:T(8,128)S(1)} custom-call(s32[1,1]{1,0:T(1,128)S(6)} %copy.6.counts, f32[2,6144,128]{2,1,0:T(8,128)} %bitcast.4, f32[6144,128]{1,0:T(8,128)} %bitcast.5), custom_call_target="tpu_custom_call" | custom-call | tf_op jit(solution)/shard_map/pallas_call | solution.py:601
  43.3 1.3 %copy.7 = f32[512,1,1024]{2,1,0:T(1,128)} copy(f32[512,1,1024]{2,1,0:T(1,128)S(1)} %bitcast.3) | data formatting | bytes 4194304

commit v5 on v4

--- a/solution.py
+++ b/solution.py
@@ -60,15 +60,25 @@
     for f in (2, 0, 1):
         loads[f].start()
     barrier = pltpu.get_barrier_semaphore()
-    for there, device in sides:
+    for there, device in sides[2:]:
         @pl.when(there)
         def _():
             pl.semaphore_signal(barrier, inc=1, device_id=device, device_id_type=MESH)
-    for off in range(2, n - 1):
-        peer = lax.rem(rank + off, n)
+    half = n // 2
+    lower = rank < half
+    base_rank = jnp.where(lower, 0, half)
+    place = rank - base_rank
+    mates = [base_rank + lax.rem(place + off, half) for off in range(1, half)]
+    asked = half - 1
+    for peer in mates:
         pl.semaphore_signal(barrier, inc=1, device_id={"curve": peer}, device_id_type=MESH)
-    for there, peer in ((has_left, n - 1), (has_right, 0)):
-        @pl.when(jnp.logical_not(there))
+    for there, device in sides[2:]:
+        asked = asked + there.astype(jnp.int32)
+    for off in (-2, -1, 1, 2):
+        peer = rank + off
+        there = (peer >= 0) & (peer < n) & (lower != (peer < half))
+        asked = asked + there.astype(jnp.int32)
+        @pl.when(there)
         def _():
             pl.semaphore_signal(barrier, inc=1, device_id={"curve": peer}, device_id_type=MESH)
 
@@ -215,7 +225,7 @@
                 packed = jnp.where(lane == spot, value, packed)
         ends[side] = packed
 
-    pl.semaphore_wait(barrier, n - 1 + has_low.astype(jnp.int32) + has_high.astype(jnp.int32))
+    pl.semaphore_wait(barrier, asked)
 
     def greeted(side):
         return pltpu.make_async_remote_copy(
@@ -243,16 +253,16 @@
         @pl.when(sides[side][0] & paired[side])
         def _():
             greeted(side).start()
-    for off in range(1, n):
+    for peer in mates:
         pltpu.make_async_remote_copy(
-            src_ref=mine, dst_ref=every.at[rank], send_sem=count_send, recv_sem=count_recv,
-            device_id={"curve": lax.rem(rank + off, n)}, device_id_type=MESH,
+            src_ref=mine, dst_ref=every.at[place], send_sem=count_send, recv_sem=count_recv,
+            device_id={"curve": peer}, device_id_type=MESH,
         ).start()
     tallies = pltpu.make_async_remote_copy(
-        src_ref=every.at[pl.ds(0, n - 1)], dst_ref=every.at[pl.ds(0, n - 1)], send_sem=count_send,
-        recv_sem=count_recv, device_id={"curve": lax.rem(rank + 1, n)}, device_id_type=MESH,
+        src_ref=every.at[pl.ds(0, half - 1)], dst_ref=every.at[pl.ds(0, half - 1)], send_sem=count_send,
+        recv_sem=count_recv, device_id={"curve": mates[0]}, device_id_type=MESH,
     )
-    keep = pltpu.make_async_copy(mine, every.at[rank], local_sem.at[0])
+    keep = pltpu.make_async_copy(mine, every.at[place], local_sem.at[0])
     keep.start()
     for kind in range(2):
         send(kind)
@@ -380,10 +390,13 @@
     keep = pltpu.make_async_copy(every, every_s, local_sem.at[1])
     keep.start()
     keep.wait()
-    before = 0
-    for r in range(n):
-        before = before + jnp.where(r < rank, every_s[r, 0, 0], 0)
-    drift_prev = jnp.clip(before - rank * AVG, -HALF, HALF)
+    before, after = 0, 0
+    for r in range(half):
+        before = before + jnp.where(r < place, every_s[r, 0, 0], 0)
+        after = after + jnp.where(r > place, every_s[r, 0, 0], 0)
+    drift_next = (n - 1 - rank) * AVG - after
+    drift_prev = jnp.where(lower, before - rank * AVG, drift_next - held + AVG)
+    drift_prev = jnp.clip(drift_prev, -HALF, HALF)
     drift_next = jnp.clip(drift_prev + held - AVG, -HALF, HALF)
     base = lax.shift_right_arithmetic(-drift_prev, 7)
     part = (-drift_prev) & (LANES - 1)
@@ -605,8 +618,8 @@
         out_specs=vmem,
         scratch_shapes=[
             pltpu.VMEM((1, LANES), jnp.int32),
-            pltpu.VMEM((n, 1, LANES), jnp.int32),
-            pltpu.SMEM((n, 1, LANES), jnp.int32),
+            pltpu.VMEM((n // 2, 1, LANES), jnp.int32),
+            pltpu.SMEM((n // 2, 1, LANES), jnp.int32),
             pltpu.VMEM((2,) + tile, f32),
             pltpu.VMEM((2,) + tile, f32),
         ]

time: 44.9 us -> 44.5 us (level)
  no operation moved by 1% of the time
where the time goes in v5:
time: 44.5 us; the launch traced here: 44.4 us
  Pallas kernels  42.4 us (95%)
  local copies, waits for them, and re-layouts  1.32 us (3%)
  between operations  0.66 us (1%)
    pallas_call x1, Pallas kernels, local(): pl.pallas_call(functools.partial(exchange, n, groups, rows), out_shape=ja...  42.4 us
    unnamed x1, local copies, waits for them, and re-layouts  1.32 us

profile of v5, /device:TPU:12, one launch (start us, length us, event | category | flops | bytes accessed | tf_op | source)
XLA Modules:
  0.0 44.4 jit_solution(384790470779518413)
XLA Ops:
  0.7 42.4 %shard_map.37 = f32[4096,128]{1,0:T(8,128)S(1)} custom-call(s32[1,1]{1,0:T(1,128)S(6)} %copy.6.counts, f32[2,6144,128]{2,1,0:T(8,128)} %bitcast.4, f32[6144,128]{1,0:T(8,128)} %bitcast.5), custom_call_target="tpu_custom_call" | custom-call | tf_op jit(solution)/shard_map/pallas_call | solution.py:614
  43.0 1.3 %copy.7 = f32[512,1,1024]{2,1,0:T(1,128)} copy(f32[512,1,1024]{2,1,0:T(1,128)S(1)} %bitcast.3) | data formatting | bytes 4194304

commit v6 on v5

--- a/solution.py
+++ b/solution.py
@@ -154,26 +154,29 @@
         return (owner if side == 0 else n - 1 - owner) // 2 * (SIDE + 1) // steps
 
     def lent(c, side):
-        start, count = message(8 + c)
+        start, count = message(6 + c)
         return pltpu.make_async_remote_copy(
             src_ref=put.at[side, pl.ds(start, count)], dst_ref=via.at[c],
-            send_sem=send_sem.at[3 * side + 2], recv_sem=via_recv.at[c],
+            send_sem=send_sem.at[3 * side + min(c, 2)], recv_sem=via_recv.at[c],
             device_id=sides[1 - side][1], device_id_type=MESH,
         )
 
     def passed(c, side):
-        start, count = message(8 + c)
+        start, count = message(6 + c)
         return pltpu.make_async_remote_copy(
             src_ref=via.at[c], dst_ref=got.at[1 - side, pl.ds(start, count)],
-            send_sem=via_send.at[c], recv_sem=recv_sem.at[side * KINDS + 8 + c],
+            send_sem=via_send.at[c], recv_sem=recv_sem.at[side * KINDS + 6 + c],
             device_id=beyond[side], device_id_type=MESH,
         )
 
+    def taken(c, side, owner):
+        return theres[c] & (routed(side, owner) > SIDE) if c < 2 else c - 2 < routed(side, owner) - 2 * side * (routed(side, owner) > SIDE)
+
     def lending(c, side):
-        return sides[side][0] & across[side] & (c < routed(side, rank))
+        return sides[side][0] & across[side] & taken(c, side, rank)
 
     def passing(c, side):
-        return passes[side] & (c < routed(side, rank - 1 + 2 * side))
+        return passes[side] & taken(c, side, rank - 1 + 2 * side)
 
     def send(kind, only=(True, True)):
         for side in range(2):
@@ -351,8 +354,15 @@
         for p in range(2):
             pack(MIDDLE + p * SIDE + x, first_of, x, outer[p])
     spread(4, step)
-    for kind in range(4, 8):
+    for kind in range(4, 6):
         send(kind)
+    for c in range(2):
+        for side in range(2):
+            @pl.when(lending(c, side))
+            def _():
+                lent(c, side).start()
+    for kind in range(6, 8):
+        send(kind, [jnp.logical_not(across[side] & (routed(side, rank) > SIDE)) for side in range(2)])
 
     def moved(met_end, own_end):
         near = pltpu.roll(met_end, LANES - SIDE, 1)
@@ -370,7 +380,7 @@
         for y in range(SIDE):
             pack(FINAL + x * SIDE + y, second_of, x, y)
     spread(2, step)
-    for c in range(SIDE):
+    for c in range(2, SIDE + 2):
         for side in range(2):
             @pl.when(lending(c, side))
             def _():
@@ -381,7 +391,7 @@
     def release(early):
         for c in range(SIDE):
             for side in range(2):
-                @pl.when(sides[side][0] & jnp.where(across[side], (c >= routed(side, rank)) & early, early == (c < soon)))
+                @pl.when(sides[side][0] & jnp.where(across[side], jnp.logical_not(taken(c + 2, side, rank)) & early, early == (c < soon)))
                 def _():
                     sent(8 + c, side).start()
     release(True)
@@ -522,7 +532,7 @@
                 for i in range(OWN):
                     change[p, 1, x, i] = lines[i] * fix[p, x + 1, i]
             spread(4, step)
-    for c in range(SIDE):
+    for c in range(SIDE + 2):
         for side in range(2):
             @pl.when(passing(c, side))
             def _():
@@ -573,7 +583,7 @@
         def _():
             greeted_on(side).wait_send()
 
-        for c in range(SIDE):
+        for c in range(SIDE + 2):
             @pl.when(passing(c, side))
             def _():
                 passed(c, side).wait_send()
@@ -627,7 +637,7 @@
         + [pltpu.SemaphoreType.DMA] * 2
         + [pltpu.SemaphoreType.DMA((k,)) for k in (2, 2, 2, 5, 6, 2 * KINDS, 4, 4, 4, 4)]
         + [pltpu.VMEM(tile, f32)] + [pltpu.SemaphoreType.DMA] * 2
-        + [pltpu.VMEM((SIDE, SIDE, WIN) + tile, f32)] + [pltpu.SemaphoreType.DMA((SIDE,))] * 2
+        + [pltpu.VMEM((SIDE + 2, SIDE, WIN) + tile, f32)] + [pltpu.SemaphoreType.DMA((SIDE + 2,))] * 2
         + [pltpu.VMEM((2 * SIDE * SIDE * rows + PAD, LANES), f32)],
         compiler_params=pltpu.CompilerParams(
             collective_id=0, has_side_effects=True, vmem_limit_bytes=50 * 1024 * 1024

time: 44.5 us -> 43.8 us (0.984)
  Pallas kernels: 42.4 us -> 41.7 us
    pallas_call x1, Pallas kernels: 42.4 us -> 41.7 us  [local(): pl.pallas_call(functools.partial(exchange, n, groups, rows), out_shape=ja...]
where the time goes in v6:
time: 43.8 us; the launch traced here: 43.7 us
  Pallas kernels  41.7 us (95%)
  local copies, waits for them, and re-layouts  1.32 us (3%)
  between operations  0.66 us (2%)
    pallas_call x1, Pallas kernels, local(): pl.pallas_call(functools.partial(exchange, n, groups, rows), out_shape=ja...  41.7 us
    unnamed x1, local copies, waits for them, and re-layouts  1.32 us

profile of v6, /device:TPU:12, one launch (start us, length us, event | category | flops | bytes accessed | tf_op | source)
XLA Modules:
  0.0 43.7 jit_solution(14054382736044157190)
XLA Ops:
  0.7 41.7 %shard_map.37 = f32[4096,128]{1,0:T(8,128)S(1)} custom-call(s32[1,1]{1,0:T(1,128)S(6)} %copy.6.counts, f32[2,6144,128]{2,1,0:T(8,128)} %bitcast.4, f32[6144,128]{1,0:T(8,128)} %bitcast.5), custom_call_target="tpu_custom_call" | custom-call | tf_op jit(solution)/shard_map/pallas_call | solution.py:624
  42.4 1.3 %copy.7 = f32[512,1,1024]{2,1,0:T(1,128)} copy(f32[512,1,1024]{2,1,0:T(1,128)S(1)} %bitcast.3) | data formatting | bytes 4194304
